TPU v7x, 32 devices: a whole 2x2x4 slice. The times are simulated.
32 devices in a mesh: row: 4 (over y, x), col: 8 (over z, core).
Axes of the slice: x: 2, y: 2, z: 4, core: 2. Of those that a mesh axis runs over, the one named last changes fastest.
Arguments:
- factors: float32 [1, 8192, 8192], P(None, 'row', 'col'), may hold values from -20 to 30, as said below
Outputs:
- refreshed: float32 [1, 8192, 8192], P(None, 'row', 'col')
Inputs may be any that keep to these rules, and one draw needn't show every extreme that they name: `factors`: every factor is symmetric positive definite.
All inputs are finite; a program needn't handle non-finite values.
Results may differ from a plain program's by a relative error of at most 0.0003.
Values sent between devices are 32-bit elements; how exact they have to be, the bound alone decides.
No kernel may reach another device: no remote copies, remote signals or barrier semaphores. Data moves between devices by JAX's collectives and lax.ppermute only.
A program may use at most 64 MiB of HBM per device.

v0:
```python
import jax
import jax.numpy as jnp
from jax import lax
from jax.sharding import PartitionSpec as P

P_SIZE = 512
STEPS = 2


damping_share = 0.03162277660168379
top_precision = lax.Precision.HIGHEST


def on_device(factors):
    members, rows_dev, cols_dev = factors.shape
    col_count = lax.axis_size("col")
    order = rows_dev * lax.axis_size("row")
    row_id = lax.axis_index("row")
    col_id = lax.axis_index("col")
    blocks_per_row = rows_dev // cols_dev
    panel_slab = P_SIZE // col_count
    diag_height = blocks_per_row * panel_slab
    row_global = row_id * rows_dev + jnp.arange(rows_dev, dtype=jnp.int32)
    col_global = col_id * cols_dev + jnp.arange(cols_dev, dtype=jnp.int32)
    row_panel = row_global % cols_dev // panel_slab
    col_panel = col_global % cols_dev // panel_slab
    on_diagonal = (row_global[:, None] == col_global[None, :])[None]
    local_trace = jnp.sum(jnp.where(on_diagonal, factors, 0.0), axis=(1, 2))
    full_trace = lax.psum(local_trace, ("row", "col"))
    working = factors + jnp.where(
        on_diagonal, (damping_share * full_trace / order)[:, None, None], 0.0
    )
    identity = jnp.broadcast_to(jnp.eye(P_SIZE, dtype=jnp.float32), (members, P_SIZE, P_SIZE))
    for section_no in range(STEPS):
        col_first = section_no * panel_slab
        panel_cols = working[:, :, col_first : col_first + panel_slab]
        diag_piece = panel_cols.reshape(members, blocks_per_row, cols_dev, panel_slab)
        diag_piece = diag_piece[:, :, col_first : col_first + panel_slab, :].reshape(
            members, diag_height, panel_slab
        )
        gathered = lax.all_gather(diag_piece[None], ("row", "col"), axis=0, tiled=True)
        gathered = gathered.reshape(
            P_SIZE // diag_height, col_count, members, diag_height, panel_slab
        )
        diag_block = gathered.transpose(2, 0, 3, 1, 4).reshape(members, P_SIZE, P_SIZE)
        factor_kk = jnp.linalg.cholesky(diag_block)
        inverse_kk = jax.scipy.linalg.solve_triangular(factor_kk, identity, lower=True)
        solve_w = jnp.swapaxes(inverse_kk, 1, 2)
        lower_rows = jnp.einsum(
            "fij,fjq->fiq",
            lax.all_gather(panel_cols, "col", axis=2, tiled=True),
            solve_w,
            precision=top_precision,
        )
        upper_rows = working.reshape(members, blocks_per_row, cols_dev, cols_dev)
        upper_rows = upper_rows[:, :, col_first : col_first + panel_slab, :].reshape(
            members, diag_height, cols_dev
        )
        cross_rows = jnp.einsum(
            "fpj,fpq->fjq",
            lax.all_gather(upper_rows, "row", axis=1, tiled=True),
            solve_w,
            precision=top_precision,
        )
        syrk_term = jnp.einsum("fiq,fjq->fij", lower_rows, cross_rows, precision=top_precision)
        trailing = ((row_panel > section_no)[:, None] & (col_panel > section_no)[None, :])[None]
        working = jnp.where(trailing, working - syrk_term, working)
        new_columns = lax.dynamic_slice_in_dim(lower_rows, col_id * panel_slab, panel_slab, 2)
        chol_rows = lax.dynamic_slice_in_dim(factor_kk, row_id * diag_height, diag_height, 1)
        chol_rows = lax.dynamic_slice_in_dim(chol_rows, col_id * panel_slab, panel_slab, 2)
        new_columns = new_columns.reshape(members, blocks_per_row, cols_dev, panel_slab)
        new_columns = new_columns.at[:, :, col_first : col_first + panel_slab, :].set(
            chol_rows.reshape(members, blocks_per_row, panel_slab, panel_slab)
        )
        new_columns = new_columns.reshape(members, rows_dev, panel_slab)
        old_columns = working[:, :, col_first : col_first + panel_slab]
        new_columns = jnp.where((row_panel >= section_no)[None, :, None], new_columns, old_columns)
        working = working.at[:, :, col_first : col_first + panel_slab].set(new_columns)
        upper_mask = ((row_panel == section_no)[:, None] & (col_panel > section_no)[None, :])[None]
        working = jnp.where(upper_mask, 0.0, working)
    return working


def solution(mesh):
    placed = (P(None, "row", "col"),)
    return jax.shard_map(
        on_device, mesh=mesh, in_specs=placed, out_specs=P(None, "row", "col"), check_vma=False
    )
```

profile of v0, /device:TPU:0, one launch (start us, length us, event | category | flops | bytes accessed | tf_op | source)
XLA Modules:
  0.0 588.8 jit_solution(5774043104662573646)
XLA Ops:
  6.5 9.1 %copy.31 = f32[1,2048,1024]{1,2,0:T(8,128)} copy(f32[1,2048,1024]{2,1,0:T(8,128)} %param.12) | data formatting | bytes 16777216 | tf_op args[0]
  15.7 5.4 fusion
  21.1 42.2 %psum.7 = f32[1]{0:T(128)} all-reduce(f32[1]{0:T(128)} %bitcast), channel_id=1, replica_groups=mesh['row'=4,'col'=8] {'row','col'}, use_global_device_ids=true, to_apply=%region_1.2 | all-reduce | flops 1 | bytes 8 | tf_op jit(solution)/shard_map/psum | solution.py:29
  63.9 4.1 fusion.1
  68.0 3.4 copy-done
  72.6 9.3 %copy.51 = f32[1,2048,1024]{2,1,0:T(8,128)} copy(f32[1,2048,1024]{1,2,0:T(8,128)} %copy-done) | data formatting | bytes 16777216 | tf_op jit(solution)/shard_map/reshape | solution.py:55
  81.9 1.9 slice.229
  85.0 41.5 %all-gather.9.cloned.1.call-done = f32[32,1,128,64]{2,3,1,0:T(8,128)} async-done(((f32[1,1,128,64]{2,3,1,0:T(8,128)}), f32[32,1,128,64]{2,3,1,0:T(8,128)}) %all-gather.9.cloned.1.call-update) | async-done | bytes 1048592 | tf_op jit(solution)/shard_map/all_gather | solution.py:41
  126.6 1.9 copy.32
  130.5 11.7 %custom-call.35 = f32[1,128,128]{2,1,0:T(8,128)S(1)} custom-call(f32[1,128,128]{2,1,0:T(8,128)S(1)} %cholesky.425), custom_call_target="Cholesky" | custom-call | tf_op jit(solution)/shard_map/jit(cholesky)/cholesky | solution.py:46
  142.2 9.8 %custom-call.36 = f32[1,1,128,128]{2,3,1,0:T(8,128)S(1)} custom-call(f32[1,1,128,128]{3,2,1,0:T(8,128)S(1)} %get-tuple-element.114), custom_call_target="InvertDiagBlocksLowerTriangular" | custom-call | tf_op jit(solution)/shard_map/jit(cholesky)/cholesky | solution.py:46
  153.5 1.4 fusion.10
  155.0 12.1 %custom-call.37 = f32[1,128,128]{2,1,0:T(8,128)S(1)} custom-call(f32[1,128,128]{2,1,0:T(8,128)S(1)} %cholesky.429), custom_call_target="Cholesky" | custom-call | tf_op jit(solution)/shard_map/jit(cholesky)/cholesky | solution.py:46
  167.2 9.8 %custom-call.38 = f32[1,1,128,128]{2,3,1,0:T(8,128)S(1)} custom-call(f32[1,1,128,128]{3,2,1,0:T(8,128)S(1)} %get-tuple-element.111), custom_call_target="InvertDiagBlocksLowerTriangular" | custom-call | tf_op jit(solution)/shard_map/jit(cholesky)/cholesky | solution.py:46
  178.6 11.7 %custom-call.39 = f32[1,128,128]{2,1,0:T(8,128)S(1)} custom-call(f32[1,128,128]{2,1,0:T(8,128)S(1)} %cholesky.434), custom_call_target="Cholesky" | custom-call | tf_op jit(solution)/shard_map/jit(cholesky)/cholesky | solution.py:46
  190.4 9.8 %custom-call.40 = f32[1,1,128,128]{2,3,1,0:T(8,128)S(1)} custom-call(f32[1,1,128,128]{3,2,1,0:T(8,128)S(1)} %get-tuple-element.108), custom_call_target="InvertDiagBlocksLowerTriangular" | custom-call | tf_op jit(solution)/shard_map/jit(cholesky)/cholesky | solution.py:46
  201.6 11.9 %custom-call.41 = f32[1,128,128]{2,1,0:T(8,128)S(1)} custom-call(f32[1,128,128]{2,1,0:T(8,128)S(1)} %fusion.18), custom_call_target="Cholesky" | custom-call | tf_op jit(solution)/shard_map/jit(cholesky)/cholesky | solution.py:46
  219.2 7.7 %while.8 = (s32[]{:T(128)}, f32[512,512]{1,0:T(8,128)S(1)}, s32[4,2]{0,1:T(2,128)S(1)}, f32[4,128,128]{2,1,0:T(8,128)S(1)}, s32[]{:T(128)}) while((s32[]{:T(128)}, f32[512,512]{1,0:T(8,128)S(1)}, s32[4,2]{0,1:T(2,128)S(1)}, f32[4,128,128]{2,1,0:T(8,128)S(1)}, s32[]{:T(128)}) %tuple.71), condition=%wide.while_cond.4, body=%wide.while_body.4.sunk | while | flops 2 | bytes 131181 | solution.py:47
  226.9 39.3 %custom-call.42 = f32[4,128,128]{1,2,0:T(8,128)S(1)} custom-call(f32[4,128,128]{2,1,0:T(8,128)S(1)} %get-tuple-element.69), custom_call_target="InvertDiagBlocksLowerTriangular" | custom-call | tf_op jit(solution)/shard_map/jit(_solve_triangular)/triangular_solve | solution.py:47
  271.2 8.4 %fusion.8 = f32[1024,512]{1,0:T(8,128)S(1)} fusion(f32[1,512,1024]{2,1,0:T(8,128)} %all-gather.11.cloned.1.call-done, f32[128,512]{1,0:T(8,128)} %fusion.53, f32[128,512]{1,0:T(8,128)} %copy-done.11, f32[128,512]{1,0:T(8,128)} %copy-done.6, f32[128,512]{1,0:T(8,128)S(1)} %fusion.42), kind=kOutput, calls=%fused_computation.18 | convolution fusion | flops 3222011904 | bytes 5242880 | tf_op jit(solution)/shard_map/fpj,fpq->fjq/dot_general | solution.py:59
  279.7 9.3 %fusion.4 = f32[2048,512]{0,1:T(8,128)S(1)} fusion(f32[1,2048,512]{1,2,0:T(8,128)} %all-gather.7.cloned.1.call-done, f32[128,512]{1,0:T(8,128)} %fusion.53, f32[128,512]{1,0:T(8,128)} %copy-done.11, f32[128,512]{1,0:T(8,128)} %copy-done.6, f32[128,512]{1,0:T(8,128)S(1)} %fusion.42), kind=kOutput, calls=%fused_computation.14 | convolution fusion | flops 6443237376 | bytes 9437184 | tf_op jit(solution)/shard_map/fij,fjq->fiq/dot_general | solution.py:49
  288.9 1.9 copy-done.3
  291.7 2.3 reshape.760
  294.0 2.2 scatter.14
  296.2 2.3 reshape.762
  298.5 18.3 %subtract_select_fusion.1 = f32[1,2048,1024]{1,2,0:T(8,128)S(1)} fusion(f32[1,2048,1024]{1,2,0:T(8,128)} %copy-done, f32[2048,512]{0,1:T(8,128)} %copy-done.3, f32[1024,512]{1,0:T(8,128)S(1)} %fusion.8, pred[2048]{0:T(1024)(128)(4,1)S(1)} %get-tuple-element.120, pred[1024]{0:T(1024)(128)(4,1)S(1)} %get-tuple-element.122), kind=kOutput, calls=%fused_computation.5 | convolution fusion | flops 12891193344 | bytes 23071744 | tf_op jit(solution)/shard_map/fiq,fjq->fij/dot_general | solution.py:65
  317.8 3.4 copy-done.1
  322.6 9.3 %copy.53 = f32[1,2048,1024]{2,1,0:T(8,128)} copy(f32[1,2048,1024]{1,2,0:T(8,128)} %copy-done.1) | data formatting | bytes 16777216 | tf_op jit(solution)/shard_map/reshape | solution.py:55
  331.9 1.9 slice.233
  334.4 41.1 %all-gather.15.cloned.1.call-done = f32[32,1,128,64]{2,3,1,0:T(8,128)} async-done(((f32[1,1,128,64]{2,3,1,0:T(8,128)}), f32[32,1,128,64]{2,3,1,0:T(8,128)}) %all-gather.15.cloned.1.call-update) | async-done | bytes 1048592 | tf_op jit(solution)/shard_map/all_gather | solution.py:41
  375.5 1.9 copy.39
  379.4 11.7 %custom-call.43 = f32[1,128,128]{2,1,0:T(8,128)S(1)} custom-call(f32[1,128,128]{2,1,0:T(8,128)S(1)} %cholesky.438), custom_call_target="Cholesky" | custom-call | tf_op jit(solution)/shard_map/jit(cholesky)/cholesky | solution.py:46
  391.3 9.8 %custom-call.44 = f32[1,1,128,128]{2,3,1,0:T(8,128)S(1)} custom-call(f32[1,1,128,128]{3,2,1,0:T(8,128)S(1)} %get-tuple-element.104), custom_call_target="InvertDiagBlocksLowerTriangular" | custom-call | tf_op jit(solution)/shard_map/jit(cholesky)/cholesky | solution.py:46
  402.6 1.4 fusion.11
  404.1 12.1 %custom-call.45 = f32[1,128,128]{2,1,0:T(8,128)S(1)} custom-call(f32[1,128,128]{2,1,0:T(8,128)S(1)} %cholesky.442), custom_call_target="Cholesky" | custom-call | tf_op jit(solution)/shard_map/jit(cholesky)/cholesky | solution.py:46
  416.2 9.8 %custom-call.46 = f32[1,1,128,128]{2,3,1,0:T(8,128)S(1)} custom-call(f32[1,1,128,128]{3,2,1,0:T(8,128)S(1)} %get-tuple-element.101), custom_call_target="InvertDiagBlocksLowerTriangular" | custom-call | tf_op jit(solution)/shard_map/jit(cholesky)/cholesky | solution.py:46
  427.6 11.7 %custom-call.47 = f32[1,128,128]{2,1,0:T(8,128)S(1)} custom-call(f32[1,128,128]{2,1,0:T(8,128)S(1)} %cholesky.447), custom_call_target="Cholesky" | custom-call | tf_op jit(solution)/shard_map/jit(cholesky)/cholesky | solution.py:46
  439.3 9.8 %custom-call.48 = f32[1,1,128,128]{2,3,1,0:T(8,128)S(1)} custom-call(f32[1,1,128,128]{3,2,1,0:T(8,128)S(1)} %get-tuple-element.98), custom_call_target="InvertDiagBlocksLowerTriangular" | custom-call | tf_op jit(solution)/shard_map/jit(cholesky)/cholesky | solution.py:46
  450.6 11.9 %custom-call.49 = f32[1,128,128]{2,1,0:T(8,128)S(1)} custom-call(f32[1,128,128]{2,1,0:T(8,128)S(1)} %fusion.19), custom_call_target="Cholesky" | custom-call | tf_op jit(solution)/shard_map/jit(cholesky)/cholesky | solution.py:46
  468.8 7.7 %while.9 = (s32[]{:T(128)}, f32[512,512]{1,0:T(8,128)S(1)}, s32[4,2]{0,1:T(2,128)S(1)}, f32[4,128,128]{2,1,0:T(8,128)S(1)}, s32[]{:T(128)}) while((s32[]{:T(128)}, f32[512,512]{1,0:T(8,128)S(1)}, s32[4,2]{0,1:T(2,128)S(1)}, f32[4,128,128]{2,1,0:T(8,128)S(1)}, s32[]{:T(128)}) %tuple.89), condition=%wide.while_cond.4.clone, body=%wide.while_body.4.clone.sunk | while | flops 2 | bytes 131181 | solution.py:47
  476.5 39.3 %custom-call.50 = f32[4,128,128]{1,2,0:T(8,128)S(1)} custom-call(f32[4,128,128]{2,1,0:T(8,128)S(1)} %get-tuple-element.70), custom_call_target="InvertDiagBlocksLowerTriangular" | custom-call | tf_op jit(solution)/shard_map/jit(_solve_triangular)/triangular_solve | solution.py:47
  520.2 8.4 %fusion.6 = f32[1024,512]{1,0:T(8,128)S(1)} fusion(f32[1,512,1024]{2,1,0:T(8,128)} %all-gather.17.cloned.1.call-done, f32[128,512]{1,0:T(8,128)S(1)} %fusion.49, f32[128,512]{1,0:T(8,128)} %copy-done.9, f32[128,512]{1,0:T(8,128)} %copy-done.4, f32[128,512]{1,0:T(8,128)S(1)} %fusion.41), kind=kOutput, calls=%fused_computation.16 | convolution fusion | flops 3222011904 | bytes 5242880 | tf_op jit(solution)/shard_map/fpj,fpq->fjq/dot_general | solution.py:59
  528.6 8.9 %fusion.2 = f32[2048,512]{0,1:T(8,128)S(1)} fusion(f32[1,2048,512]{1,2,0:T(8,128)} %all-gather.13.cloned.1.call-done, f32[128,512]{1,0:T(8,128)S(1)} %fusion.49, f32[128,512]{1,0:T(8,128)S(1)} %copy-done.10, f32[128,512]{1,0:T(8,128)S(1)} %copy-done.5, f32[128,512]{1,0:T(8,128)S(1)} %fusion.41), kind=kOutput, calls=%fused_computation.12 | convolution fusion | flops 6443237376 | bytes 9437184 | tf_op jit(solution)/shard_map/fij,fjq->fiq/dot_general | solution.py:49
  537.5 1.9 copy-done.2
  539.9 9.7 %scatter.16 = f32[1,2,1024,64]{2,1,3,0:T(2,128)S(1)} dynamic-update-slice(f32[1,2,1024,64]{2,1,3,0:T(2,128)S(1)} %reshape.771, f32[1,2,64,64]{2,1,3,0:T(2,128)S(1)} %copy.54, s32[]{:T(128)} %constant.315.clone.1, s32[]{:T(128)} %constant.315.clone.1, s32[]{:T(128)} %constant.325.clone.1, s32[]{:T(128)} %constant.315.clone.1) | dynamic-update-slice | bytes 65540 | tf_op jit(solution)/shard_map/scatter | solution.py:72
  550.0 18.2 %subtract_select_fusion = f32[1,2048,1024]{1,2,0:T(8,128)S(1)} fusion(f32[1,2048,1024]{1,2,0:T(8,128)} %copy-done.1, f32[2048,512]{0,1:T(8,128)} %copy-done.2, f32[1024,512]{1,0:T(8,128)S(1)} %fusion.6, pred[2048]{0:T(1024)(128)(4,1)S(1)} %get-tuple-element.116, pred[1024]{0:T(1024)(128)(4,1)S(1)} %get-tuple-element.121), kind=kOutput, calls=%fused_computation.4 | convolution fusion | flops 12891193344 | bytes 23071744 | tf_op jit(solution)/shard_map/fiq,fjq->fij/dot_general | solution.py:65
  568.4 4.1 and_select_fusion.1
  572.5 9.2 %copy.46 = f32[1,2048,1024]{2,1,0:T(8,128)} copy(f32[1,2048,1024]{1,2,0:T(8,128)} %and_select_fusion.1) | data formatting | bytes 16777216 | tf_op jit(solution)/shard_map/jit(_where)/select_n | solution.py:80
  (155 shorter events, 52.3 us)
Async XLA Ops:
  6.5 120.0 %all-gather.9.cloned.1.call-start = ((), (), s32[]{:S(2)}) async-start(), calls=%async_computation.1 | async-start | bytes 1081344 | tf_op jit(solution)/shard_map/all_gather | solution.py:41
  67.9 3.4 copy-start
  71.4 10.6 %copy-start.7 = (f32[1,2048,64]{1,2,0:T(8,128)}, f32[1,2048,64]{1,2,0:T(8,128)S(1)}, u32[]{:S(2)}) copy-start(f32[1,2048,64]{1,2,0:T(8,128)S(1)} %slice.227) | copy-start | bytes 1572868
  72.6 198.6 %all-gather.11.cloned.1.call-start = ((), (), s32[]{:S(2)}) async-start(), calls=%async_computation.2 | async-start | bytes 2621440 | tf_op jit(solution)/shard_map/all_gather | solution.py:61
  83.8 195.8 %all-gather.7.cloned.1.call-start = ((), (), s32[]{:S(2)}) async-start(), calls=%async_computation | async-start | bytes 4718592 | tf_op jit(solution)/shard_map/all_gather | solution.py:51
  84.6 290.9 %all-gather.15.cloned.1.call-start = ((), (), s32[]{:S(2)}) async-start(), calls=%async_computation.4 | async-start | bytes 1081344 | tf_op jit(solution)/shard_map/all_gather | solution.py:41
  129.5 1.0 copy-start.12
  268.5 0.9 copy-start.6
  269.4 0.7 copy-start.11
  288.9 1.9 copy-start.3
  298.5 18.3 %copy-start.14 = (f32[1,2048,64]{1,2,0:T(8,128)S(1)}, f32[1,2048,64]{1,2,0:T(8,128)}, u32[]{:S(2)}) copy-start(f32[1,2048,64]{1,2,0:T(8,128)} %reshape.762) | copy-start | bytes 1572868
  317.8 3.4 copy-start.1
  321.3 10.7 %copy-start.8 = (f32[1,2048,64]{1,2,0:T(8,128)}, f32[1,2048,64]{1,2,0:T(8,128)S(1)}, u32[]{:S(2)}) copy-start(f32[1,2048,64]{1,2,0:T(8,128)S(1)} %slice.231) | copy-start | bytes 1572868
  322.6 197.6 %all-gather.17.cloned.1.call-start = ((), (), s32[]{:S(2)}) async-start(), calls=%async_computation.5 | async-start | bytes 2621440 | tf_op jit(solution)/shard_map/all_gather | solution.py:61
  333.8 194.7 %all-gather.13.cloned.1.call-start = ((), (), s32[]{:S(2)}) async-start(), calls=%async_computation.3 | async-start | bytes 4718592 | tf_op jit(solution)/shard_map/all_gather | solution.py:51
  378.4 1.0 copy-start.13
  518.1 1.5 copy-start.4
  519.0 0.7 copy-start.9
  520.1 8.5 %copy-start.5 = (f32[128,512]{1,0:T(8,128)S(1)}, f32[128,512]{1,0:T(8,128)}, u32[]{:S(2)}) copy-start(f32[128,512]{1,0:T(8,128)} %copy-done.4) | copy-start | bytes 786436
  520.1 8.5 %copy-start.10 = (f32[128,512]{1,0:T(8,128)S(1)}, f32[128,512]{1,0:T(8,128)}, u32[]{:S(2)}) copy-start(f32[128,512]{1,0:T(8,128)} %copy-done.9) | copy-start | bytes 786436
  537.5 1.9 copy-start.2
Sparse Core Ops, SparseCore 0:
  72.7 53.7 all-gather.8
  128.4 34.5 all-gather.10
  164.6 47.0 all-gather.6
  322.7 52.7 all-gather.14
  377.2 34.4 all-gather.16
  413.2 47.0 all-gather.12
where the time goes:
time: 594 us; the launch traced here: 589 us
  other arithmetic  255 us (43%)
  local copies, waits for them, and re-layouts  97.5 us (16%)
  matrix products  89.8 us (15%)
  waiting for transfers between devices  83.8 us (14%)
  blocking collectives  42.2 us (7%)
  between operations  19.8 us (3%)
    another operation x29, other arithmetic, on_device(): factor_kk = jnp.linalg.cholesky(diag_block)  158 us
    all_gather x2, waiting for transfers between devices, on_device(): lax.all_gather(diag_piece[None], ('row', 'col'), axis=0, tiled=True)  82.6 us
    another operation x5, other arithmetic, on_device(): jax.scipy.linalg.solve_triangular(factor_kk, identity, lower=True)  81.2 us
    psum x1, blocking collectives, on_device(): full_trace = lax.psum(local_trace, ('row', 'col'))  42.2 us
    dot_general x2, matrix products, on_device(): jnp.einsum('fiq,fjq->fij', lower_rows, cross_rows, precision=top_precision)  36.5 us
    unnamed x31, local copies, waits for them, and re-layouts  21.9 us
    reshape x2, local copies, waits for them, and re-layouts, on_device(): upper_rows = working.reshape(members, blocks_per_row, cols_dev, cols_dev)  18.6 us
    dot_general x2, matrix products, on_device(): jnp.einsum('fij,fjq->fiq', lax.all_gather(panel_cols, 'col', axis=2, tile...  18.2 us
  transfers between devices with their start and end apart: 6, of which 2 were waited for; matrix products, arithmetic and copies ran while one was open for 55% of the time, Pallas kernels for 0%

commit v1 on v0

v1 whole, which is shorter than its diff:
```python
import jax
import jax.numpy as jnp
from jax import lax
from jax.experimental import pallas as pl
from jax.experimental.pallas import tpu as pltpu
from jax.sharding import PartitionSpec as P

P_SIZE = 512
STEPS = 2
BLK = 128
SUB = 8

damping_share = 0.03162277660168379
f32 = jnp.float32
bf16 = jnp.bfloat16


def split(x):
    hi = x.astype(bf16)
    return hi, (x - hi.astype(f32)).astype(bf16)


def dot3(a, b, dims=((1,), (0,))):
    (ah, al), (bh, bl) = a, b
    dn = (dims, ((), ()))
    out = lax.dot_general(ah, bh, dn, preferred_element_type=f32)
    out += lax.dot_general(ah, bl, dn, preferred_element_type=f32)
    return out + lax.dot_general(al, bh, dn, preferred_element_type=f32)


def factor_block(block, lane, sub):
    groups = BLK // SUB
    rows = [block[SUB * i : SUB * (i + 1), :] for i in range(groups)]
    upper, inverse = [], []
    row_of = lambda x, k: jnp.broadcast_to(x[k : k + 1, :], (SUB, BLK))
    col_of = lambda x, j: jnp.broadcast_to(x[:, j : j + 1], (SUB, BLK))
    for g in range(groups):
        first = SUB * g
        v = rows[g]
        cols = [col_of(v, first + k) for k in range(SUB)]
        raw = [[col_of(rows[i], first + k) for k in range(SUB)] for i in range(g + 1, groups)]
        va = jnp.where(lane >= first, v, 0.0)
        vb = jnp.where(lane < first, v, jnp.where(lane == sub + first, 1.0, 0.0))
        ra = jnp.zeros((SUB, BLK), f32)
        rb = jnp.zeros((SUB, BLK), f32)
        for k in range(SUB):
            pivot = row_of(cols[k], k)
            root = lax.rsqrt(pivot)
            recip = 1.0 / pivot
            here = sub == k
            ka, kb = row_of(va, k), row_of(vb, k)
            ra = jnp.where(here, ka * root, ra)
            rb = jnp.where(here, kb * root, rb)
            na, nb = ka * recip, kb * recip
            va = jnp.where(here, na, va - cols[k] * na)
            vb = jnp.where(here, nb, vb - cols[k] * nb)
            for m in range(k + 1, SUB):
                nm = row_of(cols[m], k) * recip
                cols[m] = jnp.where(here, nm, cols[m] - cols[k] * nm)
        upper.append(jnp.where(lane >= sub + first, ra, 0.0))
        inverse.append(jnp.where(lane <= sub + first, rb, 0.0))
        y = jnp.where(lane < first + SUB, vb, va)
        ys = [row_of(y, k) for k in range(SUB)]
        inside = (lane >= first) & (lane < first + SUB)
        for i in range(g + 1, groups):
            t = jnp.where(inside, 0.0, rows[i])
            for k in range(SUB):
                t = t - raw[i - g - 1][k] * ys[k]
            rows[i] = t
    return jnp.concatenate(upper, 0), jnp.concatenate(inverse, 0)


def factor_kernel(pieces, traces, lower, inv_hi, inv_lo, damp_out, w, diag_u, *, order, col_count, slab, assembled):
    n = STEPS * P_SIZE
    nb = n // BLK
    lane = lax.broadcasted_iota(jnp.int32, (SUB, BLK), 1)
    sub = lax.broadcasted_iota(jnp.int32, (SUB, BLK), 0)
    total = jnp.sum(traces[...]) * (1.0 / BLK)
    damp = damping_share * total / order
    damp_out[...] = jnp.full(damp_out.shape, damp, f32)
    if assembled:
        w[...] = pieces[...]
    else:
        for crow in range(col_count):
            for k in range(STEPS):
                top = k * P_SIZE + crow * slab
                per = pieces.shape[1] // (STEPS * slab)
                dev0 = crow // per * col_count
                begin = crow % per * STEPS * slab + k * slab
                for kk in range(STEPS):
                    parts = [
                        pieces[dev0 + c, begin : begin + slab, kk * slab : (kk + 1) * slab]
                        for c in range(col_count)
                    ]
                    w[top : top + slab, kk * P_SIZE : (kk + 1) * P_SIZE] = jnp.concatenate(parts, 1)
    eye = lax.broadcasted_iota(jnp.int32, (BLK, BLK), 0) == lax.broadcasted_iota(jnp.int32, (BLK, BLK), 1)
    for k in range(nb):
        at = slice(k * BLK, (k + 1) * BLK)
        w[at, at] = w[at, at] + jnp.where(eye, damp, 0.0)

    def step(k, _):
        here = pl.ds(pl.multiple_of(k * BLK, BLK), BLK)
        up, inv = factor_block(w[here, here], lane, sub)
        diag_u[here, :] = up
        w[here, :] = jnp.dot(inv, w[here, :], precision=lax.Precision.HIGHEST, preferred_element_type=f32)
        w[here, here] = inv

        def update(i, _):
            there = pl.ds(pl.multiple_of(i * BLK, BLK), BLK)
            left = w[here, there]
            w[there, here] = jnp.zeros((BLK, BLK), f32)
            w[there, :] = w[there, :] - lax.dot_general(
                left, w[here, :], (((0,), (0,)), ((), ())),
                precision=lax.Precision.HIGHEST, preferred_element_type=f32,
            )
            return 0

        lax.fori_loop(k + 1, nb, update, 0)
        return 0

    lax.fori_loop(0, nb, step, 0)
    for i in range(nb):
        ri = slice(i * BLK, (i + 1) * BLK)
        for j in range(nb):
            rj = slice(j * BLK, (j + 1) * BLK)
            if j <= i:
                lower[ri, rj] = (diag_u[ri, :] if i == j else w[rj, ri]).T
                hi, lo = split(w[ri, rj].T)
                inv_hi[rj, ri] = hi
                inv_lo[rj, ri] = lo
            else:
                lower[ri, rj] = jnp.zeros((BLK, BLK), f32)
                inv_hi[rj, ri] = jnp.zeros((BLK, BLK), bf16)
                inv_lo[rj, ri] = jnp.zeros((BLK, BLK), bf16)


def apply_kernel(
    coords, panel, cross, inv_hi, inv_lo, own_hi, own_lo, own_low, damp, work, out, cr, ch, cl, *, slab, cols_dev, rows_dev
):
    t = pl.program_id(0)
    tile = work.shape[0]
    col_count = panel.shape[0]
    width = STEPS * slab
    inverse = (inv_hi[...], inv_lo[...])

    @pl.when(t == 0)
    def _():
        for c in range(col_count):
            for k in range(STEPS):
                cr[k * P_SIZE + c * slab : k * P_SIZE + (c + 1) * slab, :] = cross[
                    c * width + k * slab : c * width + (k + 1) * slab, :
                ]
        hi, lo = split(dot3(inverse, split(cr[...]), ((0,), (0,))))
        ch[...] = hi
        cl[...] = lo

    rows = jnp.concatenate(
        [panel[c, :, k * slab : (k + 1) * slab] for k in range(STEPS) for c in range(col_count)], 1
    )
    rows = split(rows)
    left = split(dot3(rows, inverse))
    own = dot3(rows, (own_hi[...], own_lo[...]))
    update = dot3(left, (ch[...], cl[...]))
    row = lax.broadcasted_iota(jnp.int32, work.shape, 0) + (coords[0] * rows_dev + t * tile)
    col = lax.broadcasted_iota(jnp.int32, work.shape, 1) + coords[1] * cols_dev
    out[...] = work[...] + jnp.where(row == col, damp[0:1, 0:1], 0.0) - update
    out[:, 0:width] = own
    per = cols_dev // tile

    @pl.when(t % per == 0)
    def _():
        out[0:width, :] = jnp.zeros((width, cols_dev), f32)
        begin = pl.multiple_of(t // per * width, width)
        out[0:width, 0:width] = own_low[pl.ds(begin, width), :]


def on_device(factors):
    members, rows_dev, cols_dev = factors.shape
    col_count = lax.axis_size("col")
    row_count = lax.axis_size("row")
    order = rows_dev * row_count
    row_id = lax.axis_index("row")
    col_id = lax.axis_index("col")
    per_row = rows_dev // cols_dev
    slab = P_SIZE // col_count
    width = STEPS * slab
    n = STEPS * P_SIZE
    outs = []
    for member in range(members):
        local = factors[member]
        tall = local[:, :width]
        piece = jnp.concatenate([tall[b * cols_dev : b * cols_dev + width] for b in range(per_row)], 0)
        start = (col_id % per_row) * cols_dev
        on_diag = jnp.eye(BLK, dtype=f32) * (col_id // per_row == row_id)
        acc = jnp.zeros((BLK, BLK), f32)
        for b in range(cols_dev // BLK):
            acc += on_diag * lax.dynamic_slice(local, (start + b * BLK, b * BLK), (BLK, BLK))
        height = per_row * width
        assembled = slab % 64 != 0
        if assembled:
            traces = jnp.full((SUB, BLK), lax.psum(jnp.sum(acc), ("row", "col")) / SUB)
            pieces = lax.all_gather(piece, "col", axis=1, tiled=True)
            pieces = lax.all_gather(pieces, "row", axis=0, tiled=True)
            sequence = jnp.arange(n).reshape(col_count, STEPS, slab).transpose(1, 0, 2).reshape(n)
            pieces = jnp.take(jnp.take(pieces, sequence, axis=0).T, sequence, axis=0).T
        else:
            extra = jnp.broadcast_to(jnp.sum(acc), (SUB, width))
            pieces = lax.all_gather(jnp.concatenate([piece, extra], 0), ("row", "col"), axis=0)
            traces = jnp.broadcast_to(pieces[:, height, :1], (row_count * col_count, BLK))
        wide = jnp.concatenate([local[b * cols_dev : b * cols_dev + width] for b in range(per_row)], 0)
        panel = lax.all_gather(tall, "col", axis=0)
        cross = lax.all_gather(wide, "row", axis=0, tiled=True)

        def kernel(pieces, *rest):
            factor_kernel(
                pieces, *rest, order=order, col_count=col_count, slab=slab, assembled=assembled
            )

        if not assembled:
            def kernel(pieces, *rest, height=height):
                factor_kernel(
                    pieces.at[:, 0:height, :], *rest,
                    order=order, col_count=col_count, slab=slab, assembled=False,
                )

        lower, inv_hi, inv_lo, damp = pl.pallas_call(
            kernel,
            out_shape=(
                jax.ShapeDtypeStruct((n, n), f32),
                jax.ShapeDtypeStruct((n, n), bf16),
                jax.ShapeDtypeStruct((n, n), bf16),
                jax.ShapeDtypeStruct((SUB, BLK), f32),
            ),
            scratch_shapes=[pltpu.VMEM((n, n), f32), pltpu.VMEM((n, BLK), f32)],
            compiler_params=pltpu.CompilerParams(vmem_limit_bytes=60 * 1024 * 1024),
            cost_estimate=pl.CostEstimate(flops=40_000_000_000, bytes_accessed=12_000_000, transcendentals=0),
            name="factor",
        )(pieces, traces)
        split_cols = lambda x: lax.dynamic_slice_in_dim(
            x.reshape(x.shape[0], STEPS, col_count, slab), col_id, 1, 2
        ).reshape(x.shape[0], width)
        own_hi, own_lo = split_cols(inv_hi), split_cols(inv_lo)
        own_low = lax.dynamic_slice_in_dim(
            lower.reshape(STEPS, row_count, per_row, slab, n), row_id, 1, 1
        )
        own_low = split_cols(own_low[:, 0].transpose(1, 0, 2, 3).reshape(height, n))
        coords = jnp.stack([row_id, col_id]).astype(jnp.int32)
        tile = min(256, cols_dev)
        full = lambda a: pl.BlockSpec(a.shape, lambda t: (0,) * a.ndim)
        outs.append(pl.pallas_call(
            lambda *refs: apply_kernel(*refs, slab=slab, cols_dev=cols_dev, rows_dev=rows_dev),
            grid=(rows_dev // tile,),
            in_specs=[
                pl.BlockSpec(memory_space=pltpu.SMEM),
                pl.BlockSpec((col_count, tile, width), lambda t: (0, t, 0)),
                full(cross), full(inv_hi), full(inv_lo), full(own_hi), full(own_lo), full(own_low), full(damp),
                pl.BlockSpec((tile, cols_dev), lambda t: (t, 0)),
            ],
            out_specs=pl.BlockSpec((tile, cols_dev), lambda t: (t, 0)),
            out_shape=jax.ShapeDtypeStruct((rows_dev, cols_dev), f32),
            scratch_shapes=[
                pltpu.VMEM((n, cols_dev), f32),
                pltpu.VMEM((n, cols_dev), bf16),
                pltpu.VMEM((n, cols_dev), bf16),
            ],
            compiler_params=pltpu.CompilerParams(vmem_limit_bytes=60 * 1024 * 1024),
            name="apply",
        )(coords, panel, cross, inv_hi, inv_lo, own_hi, own_lo, own_low, damp, local))
    return jnp.stack(outs)


def solution(mesh):
    placed = (P(None, "row", "col"),)
    return jax.shard_map(
        on_device, mesh=mesh, in_specs=placed, out_specs=P(None, "row", "col"), check_vma=False
    )
```

time: 594 us -> 265 us (0.45)
  other arithmetic: 255 us -> 4.11 us
  Pallas kernels: 0 us -> 113 us
  matrix products: 89.8 us -> 0 us
  local copies, waits for them, and re-layouts: 97.5 us -> 21.1 us
  blocking collectives: 42.2 us -> 0 us
  waiting for transfers between devices: 83.8 us -> 113 us
  between operations: 19.8 us -> 13.2 us
    another operation x34 -> x1, other arithmetic: 240 us -> 0.58 us  [on_device(): coords = jnp.stack([row_id, col_id]).astype(jnp.int32)]
    pallas_call x0 -> x2, Pallas kernels: none -> 113 us  [the longest x1 67.8 us: on_device(): pl.pallas_call(kernel, out_shape=(jax.ShapeDtypeStruct((n, n), f32), jax....]
    dot_general x6 -> x0, matrix products: 71.4 us -> none  [the longest x2 36.5 us: on_device(): jnp.einsum('fiq,fjq->fij', lower_rows, cross_rows, precision=top_precision)]
    psum x1 -> x0, blocking collectives: 42.2 us -> none  [on_device(): full_trace = lax.psum(local_trace, ('row', 'col'))]
    all_gather x6 -> x3, waiting for transfers between devices: 82.7 us -> 113 us  [the longest x1 59.6 us: on_device(): lax.all_gather(jnp.concatenate([piece, extra], 0), ('row', 'col'), axis=0)]
    reshape x12 -> x3, local copies, waits for them, and re-layouts: 26.4 us -> 2.45 us  [on_device(): split_cols = lambda x: lax.dynamic_slice_in_dim(x.reshape(x.shape[0], STE...]
    unnamed x31 -> x2, local copies, waits for them, and re-layouts: 21.9 us -> 0.01 us
    another operation x26 -> x0, matrix products: 18.4 us -> none  [the longest x12 11.4 us: on_device(): factor_kk = jnp.linalg.cholesky(diag_block)]
  transfers between devices with their start and end apart: 6 -> 3, of which waited for: 2 -> 2; matrix products, arithmetic and copies ran while one was open for 55% -> 8% of each run, Pallas kernels for 0% -> 26%
where the time goes in v1:
time: 265 us
  waiting for transfers between devices  113 us (43%)
  Pallas kernels  113 us (43%)
  local copies, waits for them, and re-layouts  21.1 us (8%)
  between operations  13.2 us (5%)
  other arithmetic  4.11 us (2%)
    pallas_call x1, Pallas kernels, on_device(): pl.pallas_call(kernel, out_shape=(jax.ShapeDtypeStruct((n, n), f32), jax....  67.8 us
    all_gather x1, waiting for transfers between devices, on_device(): lax.all_gather(jnp.concatenate([piece, extra], 0), ('row', 'col'), axis=0)  59.6 us
    all_gather x1, waiting for transfers between devices, on_device(): panel = lax.all_gather(tall, 'col', axis=0)  52.9 us
    pallas_call x1, Pallas kernels, on_device(): pl.pallas_call(lambda *refs: apply_kernel(*refs, slab=slab, cols_dev=cols...  45.6 us
    pallas_call x2, local copies, waits for them, and re-layouts, on_device(): pl.pallas_call(kernel, out_shape=(jax.ShapeDtypeStruct((n, n), f32), jax....  5.42 us
  transfers between devices with their start and end apart: 3, of which 2 were waited for; matrix products, arithmetic and copies ran while one was open for 8% of the time, Pallas kernels for 26%

profile of v1, /device:TPU:0, one launch (start us, length us, event | category | flops | bytes accessed | tf_op | source)
XLA Modules:
  0.0 264.6 jit_solution(13424888166182236302)
XLA Ops:
  6.5 0.0 all-gather.10.cloned.1.call-start
  6.5 0.9 fusion.1
  7.5 1.7 fusion
  9.2 0.6 broadcast_in_dim.10
  9.9 0.8 maximum_maximum_fusion
  10.6 0.0 all-gather.10.cloned.1.call-update
  10.6 0.0 all-gather.6.cloned.1.call-start
  10.7 1.3 slice_bitcast_fusion.1
  12.0 1.1 pad_maximum_fusion
  13.0 0.0 all-gather.6.cloned.1.call-update
  13.1 0.0 all-gather.8.cloned.1.call-start
  13.1 2.3 slice.34
  15.4 0.0 all-gather.8.cloned.1.call-update
  15.4 0.6 pad_add_fusion.refs_0_
  16.0 59.6 %all-gather.10.cloned.1.call-done = f32[8448,128]{1,0:T(8,128)} async-done(((f32[264,128]{1,0:T(8,128)}), f32[8448,128]{1,0:T(8,128)}) %all-gather.10.cloned.1.call-update) | async-done | bytes 4325392 | tf_op jit(solution)/shard_map/all_gather | solution.py:208
  75.7 1.2 slice_reduce_fusion
  76.9 0.7 broadcast_in_dim.12.rest_0_
  77.5 67.8 %factor.1 = (f32[1024,1024]{1,0:T(8,128)}, bf16[1024,1024]{1,0:T(8,128)(2,1)}, bf16[1024,1024]{1,0:T(8,128)(2,1)}, f32[8,128]{1,0:T(8,128)}) custom-call(f32[32,264,128]{2,1,0:T(8,128)} %bitcast.37, f32[32,128]{1,0:T(8,128)} %broadcast_in_dim.12.rest_0_), custom_call_target="tpu_custom_call" | custom-call | flops 40000000000 | bytes 12000000 | tf_op jit(solution)/shard_map/factor/pallas_call | solution.py:226
  145.4 0.0 copy-start
  145.4 1.5 copy_bitcast_fusion
  146.8 1.9 reshape_reshape.3
  148.7 1.8 constant_dynamic-slice_fusion
  150.5 0.1 copy.7
  150.6 0.7 copy.10.refs_7_
  151.4 0.0 copy-done
  151.4 2.5 copy.4
  153.9 2.9 %copy.5 = bf16[1024,1024]{0,1:T(8,128)(2,1)S(1)} copy(bf16[1024,1024]{1,0:T(8,128)(2,1)} %get-tuple-element.10.refs_4_) | data formatting | bytes 4194304 | tf_op jit(solution)/shard_map/factor/pallas_call | solution.py:226
  156.8 1.0 constant_dynamic-slice_fusion.2
  157.8 0.8 copy.9.refs_6_
  158.7 0.9 copy.8.refs_5_
  159.5 0.0 all-gather.6.cloned.1.call-done.refs_2_
  159.5 52.9 %all-gather.8.cloned.1.call-done = f32[16384,128]{1,0:T(8,128)} async-done(((f32[2048,128]{1,0:T(8,128)}), f32[16384,128]{1,0:T(8,128)}) %all-gather.8.cloned.1.call-update) | async-done | bytes 8388624 | tf_op jit(solution)/shard_map/all_gather | solution.py:211
  212.4 45.6 %apply.1 = f32[2048,1024]{1,0:T(8,128)} custom-call(s32[2]{0:T(128)} %pad_add_fusion.refs_0_, f32[8,2048,128]{2,1,0:T(8,128)} %bitcast.29, f32[1024,1024]{1,0:T(8,128)} %all-gather.6.cloned.1.call-done.refs_2_, bf16[1024,1024]{1,0:T(8,128)(2,1)} %get-tuple-element.9.refs_3_, bf16[1024,1024]{1,0:T(8,128)(2,1)} %get-tuple-element.10.refs_4_, ...), custom_call_target="tpu_custom_call" | custom-call | tf_op jit(solution)/shard_map/apply/pallas_call | solution.py:250
  (1 shorter events, 0.0 us)
Async XLA Ops:
  6.5 69.1 %all-gather.10.cloned.1.call-start = ((), (), s32[]{:S(2)}) async-start(), calls=%async_computation.2 | async-start | bytes 4460544 | tf_op jit(solution)/shard_map/all_gather | solution.py:208
  10.6 148.9 %all-gather.6.cloned.1.call-start = ((), (), s32[]{:S(2)}) async-start(), calls=%async_computation | async-start | bytes 5242880 | tf_op jit(solution)/shard_map/all_gather | solution.py:212
  13.1 199.4 %all-gather.8.cloned.1.call-start = ((), (), s32[]{:S(2)}) async-start(), calls=%async_computation.1 | async-start | bytes 9437184 | tf_op jit(solution)/shard_map/all_gather | solution.py:211
  145.4 6.0 %copy-start = (bf16[1024,1024]{1,0:T(8,128)(2,1)S(1)}, bf16[1024,1024]{1,0:T(8,128)(2,1)}, u32[]{:S(2)}) copy-start(bf16[1024,1024]{1,0:T(8,128)(2,1)} %get-tuple-element.9.refs_3_) | copy-start | bytes 6291460
Sparse Core Ops, SparseCore 0:
  10.8 64.8 all-gather.9
  77.5 51.1 all-gather.5
  130.3 82.0 all-gather.7

commit v2 on v1

--- a/solution.py
+++ b/solution.py
@@ -70,7 +70,9 @@
     return jnp.concatenate(upper, 0), jnp.concatenate(inverse, 0)
 
 
-def factor_kernel(pieces, traces, lower, inv_hi, inv_lo, damp_out, w, diag_u, *, order, col_count, slab, assembled):
+def factor_kernel(
+    pieces, traces, lower, inv_hi, inv_lo, damp_out, w, diag_u, turned, stack_l, stack_r, *, order, col_count, slab, assembled
+):
     n = STEPS * P_SIZE
     nb = n // BLK
     lane = lax.broadcasted_iota(jnp.int32, (SUB, BLK), 1)
@@ -104,14 +106,16 @@
         diag_u[here, :] = up
         w[here, :] = jnp.dot(inv, w[here, :], precision=lax.Precision.HIGHEST, preferred_element_type=f32)
         w[here, here] = inv
+        hi, lo = split(w[here, :])
+        for part, (x, y) in enumerate(((hi, hi), (hi, lo), (lo, hi))):
+            stack_l[part * BLK : (part + 1) * BLK, :] = x
+            stack_r[part * BLK : (part + 1) * BLK, :] = y
 
         def update(i, _):
             there = pl.ds(pl.multiple_of(i * BLK, BLK), BLK)
-            left = w[here, there]
             w[there, here] = jnp.zeros((BLK, BLK), f32)
             w[there, :] = w[there, :] - lax.dot_general(
-                left, w[here, :], (((0,), (0,)), ((), ())),
-                precision=lax.Precision.HIGHEST, preferred_element_type=f32,
+                stack_l[:, there], stack_r[...], (((0,), (0,)), ((), ())), preferred_element_type=f32
             )
             return 0
 
@@ -119,24 +123,46 @@
         return 0
 
     lax.fori_loop(0, nb, step, 0)
+
+    def strips(store):
+        if assembled:
+            store(slice(0, n), turned[...])
+            return
+        for c in range(col_count):
+            for k in range(STEPS):
+                top = k * P_SIZE + c * slab
+                line = turned[top : top + slab, :]
+                parts = [
+                    line[:, kk * P_SIZE + cc * slab : kk * P_SIZE + (cc + 1) * slab]
+                    for cc in range(col_count)
+                    for kk in range(STEPS)
+                ]
+                first = (c * STEPS + k) * slab
+                store(slice(first, first + slab), jnp.concatenate(parts, 1))
+
+    def store_lower(at, x):
+        lower[at, :] = x
+
+    def store_inverse(at, x):
+        inv_hi[at, :], inv_lo[at, :] = split(x)
+
+    at = lambda i: slice(i * BLK, (i + 1) * BLK)
+    turned[...] = jnp.zeros(turned.shape, f32)
     for i in range(nb):
-        ri = slice(i * BLK, (i + 1) * BLK)
-        for j in range(nb):
-            rj = slice(j * BLK, (j + 1) * BLK)
-            if j <= i:
-                lower[ri, rj] = (diag_u[ri, :] if i == j else w[rj, ri]).T
-                hi, lo = split(w[ri, rj].T)
-                inv_hi[rj, ri] = hi
-                inv_lo[rj, ri] = lo
-            else:
-                lower[ri, rj] = jnp.zeros((BLK, BLK), f32)
-                inv_hi[rj, ri] = jnp.zeros((BLK, BLK), bf16)
-                inv_lo[rj, ri] = jnp.zeros((BLK, BLK), bf16)
+        for j in range(i + 1):
+            turned[at(i), at(j)] = (diag_u[at(i), :] if i == j else w[at(j), at(i)]).T
+    strips(store_lower)
+    turned[...] = jnp.zeros(turned.shape, f32)
+    for i in range(nb):
+        for j in range(i + 1):
+            turned[at(j), at(i)] = w[at(i), at(j)].T
+    strips(store_inverse)
 
 
 def apply_kernel(
-    coords, panel, cross, inv_hi, inv_lo, own_hi, own_lo, own_low, damp, work, out, cr, ch, cl, *, slab, cols_dev, rows_dev
+    coords, panel, inv_hi, inv_lo, own_hi, own_lo, own_low, damp, work, *rest, slab, cols_dev, rows_dev
 ):
+    *cross, out, cr, ch, cl = rest
     t = pl.program_id(0)
     tile = work.shape[0]
     col_count = panel.shape[0]
@@ -145,18 +171,15 @@
 
     @pl.when(t == 0)
     def _():
-        for c in range(col_count):
-            for k in range(STEPS):
-                cr[k * P_SIZE + c * slab : k * P_SIZE + (c + 1) * slab, :] = cross[
-                    c * width + k * slab : c * width + (k + 1) * slab, :
-                ]
+        for shift, piece in enumerate(cross):
+            height = piece.shape[0]
+            begin = pl.multiple_of((coords[0] + shift) % len(cross) * height, height)
+            cr[pl.ds(begin, height), :] = piece[...]
         hi, lo = split(dot3(inverse, split(cr[...]), ((0,), (0,))))
         ch[...] = hi
         cl[...] = lo
 
-    rows = jnp.concatenate(
-        [panel[c, :, k * slab : (k + 1) * slab] for k in range(STEPS) for c in range(col_count)], 1
-    )
+    rows = jnp.concatenate([panel[c] for c in range(col_count)], 1)
     rows = split(rows)
     left = split(dot3(rows, inverse))
     own = dot3(rows, (own_hi[...], own_lo[...]))
@@ -209,7 +232,11 @@
             traces = jnp.broadcast_to(pieces[:, height, :1], (row_count * col_count, BLK))
         wide = jnp.concatenate([local[b * cols_dev : b * cols_dev + width] for b in range(per_row)], 0)
         panel = lax.all_gather(tall, "col", axis=0)
-        cross = lax.all_gather(wide, "row", axis=0, tiled=True)
+        shifted = [
+            lax.ppermute(wide, "row", [(i, (i - shift) % row_count) for i in range(row_count)])
+            for shift in range(1, row_count)
+        ]
+        cross = [wide] + shifted
 
         def kernel(pieces, *rest):
             factor_kernel(
@@ -231,41 +258,58 @@
                 jax.ShapeDtypeStruct((n, n), bf16),
                 jax.ShapeDtypeStruct((SUB, BLK), f32),
             ),
-            scratch_shapes=[pltpu.VMEM((n, n), f32), pltpu.VMEM((n, BLK), f32)],
+            scratch_shapes=[
+                pltpu.VMEM((n, n), f32),
+                pltpu.VMEM((n, BLK), f32),
+                pltpu.VMEM((n, n), f32),
+                pltpu.VMEM((3 * BLK, n), bf16),
+                pltpu.VMEM((3 * BLK, n), bf16),
+            ],
             compiler_params=pltpu.CompilerParams(vmem_limit_bytes=60 * 1024 * 1024),
             cost_estimate=pl.CostEstimate(flops=40_000_000_000, bytes_accessed=12_000_000, transcendentals=0),
             name="factor",
         )(pieces, traces)
-        split_cols = lambda x: lax.dynamic_slice_in_dim(
-            x.reshape(x.shape[0], STEPS, col_count, slab), col_id, 1, 2
-        ).reshape(x.shape[0], width)
-        own_hi, own_lo = split_cols(inv_hi), split_cols(inv_lo)
-        own_low = lax.dynamic_slice_in_dim(
-            lower.reshape(STEPS, row_count, per_row, slab, n), row_id, 1, 1
-        )
-        own_low = split_cols(own_low[:, 0].transpose(1, 0, 2, 3).reshape(height, n))
+        if assembled:
+            sequence = jnp.arange(n).reshape(STEPS, col_count, slab).transpose(1, 0, 2).reshape(n)
+            reorder = lambda x: jnp.take(jnp.take(x, sequence, axis=0).T, sequence, axis=0).T
+            lower, inv_hi, inv_lo = reorder(lower), reorder(inv_hi), reorder(inv_lo)
+            own = lambda x: lax.dynamic_slice_in_dim(x, col_id * width, width, 1)
+            own_hi, own_lo = own(inv_hi), own(inv_lo)
+            own_low = own(lax.dynamic_slice_in_dim(lower, row_id * height, height, 0))
+            own_row = own_col = lambda t, at: (0, 0)
+        else:
+            own_hi, own_lo, own_low = inv_hi, inv_lo, lower
+            own_col = lambda t, at: (0, at[1])
+            own_row = lambda t, at: (at[0], at[1])
         coords = jnp.stack([row_id, col_id]).astype(jnp.int32)
         tile = min(256, cols_dev)
-        full = lambda a: pl.BlockSpec(a.shape, lambda t: (0,) * a.ndim)
+        full = lambda a: pl.BlockSpec(a.shape, lambda t, at: (0,) * a.ndim)
         outs.append(pl.pallas_call(
             lambda *refs: apply_kernel(*refs, slab=slab, cols_dev=cols_dev, rows_dev=rows_dev),
-            grid=(rows_dev // tile,),
-            in_specs=[
-                pl.BlockSpec(memory_space=pltpu.SMEM),
-                pl.BlockSpec((col_count, tile, width), lambda t: (0, t, 0)),
-                full(cross), full(inv_hi), full(inv_lo), full(own_hi), full(own_lo), full(own_low), full(damp),
-                pl.BlockSpec((tile, cols_dev), lambda t: (t, 0)),
-            ],
-            out_specs=pl.BlockSpec((tile, cols_dev), lambda t: (t, 0)),
+            grid_spec=pltpu.PrefetchScalarGridSpec(
+                num_scalar_prefetch=1,
+                grid=(rows_dev // tile,),
+                in_specs=[
+                    pl.BlockSpec((col_count, tile, width), lambda t, at: (0, t, 0)),
+                    full(inv_hi), full(inv_lo),
+                    pl.BlockSpec((n, width), own_col),
+                    pl.BlockSpec((n, width), own_col),
+                    pl.BlockSpec((height, width), own_row),
+                    full(damp),
+                    pl.BlockSpec((tile, cols_dev), lambda t, at: (t, 0)),
+                    *[full(x) for x in cross],
+                ],
+                out_specs=pl.BlockSpec((tile, cols_dev), lambda t, at: (t, 0)),
+                scratch_shapes=[
+                    pltpu.VMEM((n, cols_dev), f32),
+                    pltpu.VMEM((n, cols_dev), bf16),
+                    pltpu.VMEM((n, cols_dev), bf16),
+                ],
+            ),
             out_shape=jax.ShapeDtypeStruct((rows_dev, cols_dev), f32),
-            scratch_shapes=[
-                pltpu.VMEM((n, cols_dev), f32),
-                pltpu.VMEM((n, cols_dev), bf16),
-                pltpu.VMEM((n, cols_dev), bf16),
-            ],
             compiler_params=pltpu.CompilerParams(vmem_limit_bytes=60 * 1024 * 1024),
             name="apply",
-        )(coords, panel, cross, inv_hi, inv_lo, own_hi, own_lo, own_low, damp, local))
+        )(coords, panel, inv_hi, inv_lo, own_hi, own_lo, own_low, damp, local, *cross))
     return jnp.stack(outs)
 
 

time: 265 us -> 232 us (0.88)
  waiting for transfers between devices: 113 us -> 94 us
  local copies, waits for them, and re-layouts: 21.1 us -> 6.98 us
  starting transfers between devices: 0.09 us -> 6.02 us
  Pallas kernels: 113 us -> 108 us
    all_gather x1, waiting for transfers between devices: 52.9 us -> 18.8 us  [on_device(): panel = lax.all_gather(tall, 'col', axis=0)]
    all_gather x1, waiting for transfers between devices: 59.6 us -> 75.1 us  [on_device(): lax.all_gather(jnp.concatenate([piece, extra], 0), ('row', 'col'), axis=0)]
    pallas_call x1, Pallas kernels: 67.8 us -> 61.4 us  [on_device(): pl.pallas_call(kernel, out_shape=(jax.ShapeDtypeStruct((n, n), f32), jax....]
    ppermute x0 -> x3, starting transfers between devices: none -> 5.97 us  [on_device(): lax.ppermute(wide, 'row', [(i, (i - shift) % row_count) for i in range(ro...]
    pallas_call x2 -> x0, local copies, waits for them, and re-layouts: 5.42 us -> none  [on_device(): pl.pallas_call(kernel, out_shape=(jax.ShapeDtypeStruct((n, n), f32), jax....]
    dynamic_slice x3 -> x0, local copies, waits for them, and re-layouts: 2.89 us -> none  [on_device(): lax.dynamic_slice_in_dim(x.reshape(x.shape[0], STEPS, col_count, slab), c...]
  transfers between devices with their start and end apart: 3 -> 5, of which waited for: 2 -> 2; matrix products, arithmetic and copies ran while one was open for 8% -> 3% of each run, Pallas kernels for 26% -> 27%
where the time goes in v2:
time: 232 us
  Pallas kernels  108 us (47%)
  waiting for transfers between devices  94 us (41%)
  between operations  13.5 us (6%)
  local copies, waits for them, and re-layouts  6.98 us (3%)
  starting transfers between devices  6.02 us (3%)
  other arithmetic  3.22 us (1%)
    all_gather x1, waiting for transfers between devices, on_device(): lax.all_gather(jnp.concatenate([piece, extra], 0), ('row', 'col'), axis=0)  75.1 us
    pallas_call x1, Pallas kernels, on_device(): pl.pallas_call(kernel, out_shape=(jax.ShapeDtypeStruct((n, n), f32), jax....  61.4 us
    pallas_call x1, Pallas kernels, on_device(): pl.pallas_call(lambda *refs: apply_kernel(*refs, slab=slab, cols_dev=cols...  46.5 us
    all_gather x1, waiting for transfers between devices, on_device(): panel = lax.all_gather(tall, 'col', axis=0)  18.8 us
    ppermute x3, starting transfers between devices, on_device(): lax.ppermute(wide, 'row', [(i, (i - shift) % row_count) for i in range(ro...  5.97 us
  transfers between devices with their start and end apart: 5, of which 2 were waited for; matrix products, arithmetic and copies ran while one was open for 3% of the time, Pallas kernels for 27%

profile of v2, /device:TPU:0, one launch (start us, length us, event | category | flops | bytes accessed | tf_op | source)
XLA Modules:
  0.0 231.7 jit_solution(16921427538990123087)
XLA Ops:
  6.5 0.0 all-gather.7.cloned.1.call-start
  6.5 0.9 fusion.1
  7.5 1.7 fusion
  9.2 0.6 broadcast_in_dim.10
  9.9 0.8 maximum_maximum_fusion
  10.6 0.0 all-gather.7.cloned.1.call-update
  10.6 0.0 all-gather.5.cloned.1.call-start
  10.7 2.3 slice.34
  13.0 0.0 all-gather.5.cloned.1.call-update
  13.0 1.3 slice_bitcast_fusion.1
  14.3 0.1 pad_maximum_fusion.refs_9_
  14.4 0.0 copy-start
  14.4 3.0 %collective-permute-start.2 = (f32[256,1024]{1,0:T(8,128)S(1)}, f32[256,1024]{1,0:T(8,128)S(1)}, u32[]{:S(2)}, u32[]{:S(2)}) collective-permute-start(f32[256,1024]{1,0:T(8,128)S(1)} %pad_maximum_fusion.refs_9_), channel_id=1, source_target_pairs={{0,8},{8,16},{16,24},{24,0},{1,9},{9,17},{17,25},{25,1},{2,10},{10... | collective-permute-start | bytes 3145736 | tf_op jit(solution)/shard_map/ppermute | solution.py:236
  17.4 1.5 collective-permute-start.1
  18.9 1.4 collective-permute-start
  20.4 0.6 pad_add_fusion.refs_0_
  21.0 75.1 %all-gather.7.cloned.1.call-done = f32[8448,128]{1,0:T(8,128)} async-done(((f32[264,128]{1,0:T(8,128)}), f32[8448,128]{1,0:T(8,128)}) %all-gather.7.cloned.1.call-update) | async-done | bytes 4325392 | tf_op jit(solution)/shard_map/all_gather | solution.py:231
  96.1 1.2 slice_reduce_fusion
  97.3 0.7 broadcast_in_dim.12.rest_0_
  98.0 61.4 %factor.1 = (f32[1024,1024]{1,0:T(8,128)}, bf16[1024,1024]{1,0:T(8,128)(2,1)}, bf16[1024,1024]{1,0:T(8,128)(2,1)}, f32[8,128]{1,0:T(8,128)}) custom-call(f32[32,264,128]{2,1,0:T(8,128)} %bitcast.19, f32[32,128]{1,0:T(8,128)} %broadcast_in_dim.12.rest_0_), custom_call_target="tpu_custom_call" | custom-call | flops 40000000000 | bytes 12000000 | tf_op jit(solution)/shard_map/factor/pallas_call | solution.py:253
  159.5 0.0 copy-done
  159.5 0.0 collective-permute-done.2.refs_12_
  159.5 0.0 copy-start.1
  159.5 0.0 collective-permute-done.1.refs_11_
  159.5 0.0 copy-start.2
  159.5 0.0 collective-permute-done.refs_10_
  159.5 18.8 %all-gather.5.cloned.1.call-done = f32[16384,128]{1,0:T(8,128)} async-done(((f32[2048,128]{1,0:T(8,128)}), f32[16384,128]{1,0:T(8,128)}) %all-gather.5.cloned.1.call-update) | async-done | bytes 8388624 | tf_op jit(solution)/shard_map/all_gather | solution.py:234
  178.3 0.0 copy-done.1
  178.3 0.0 copy-done.2
  178.3 46.5 %apply.1 = f32[2048,1024]{1,0:T(8,128)} custom-call(s32[2]{0:T(128)} %pad_add_fusion.refs_0_, f32[8,2048,128]{2,1,0:T(8,128)} %bitcast.17, bf16[1024,1024]{1,0:T(8,128)(2,1)} %get-tuple-element.9.refs_2_.refs_4_, bf16[1024,1024]{1,0:T(8,128)(2,1)} %get-tuple-element.10.refs_3_.refs_5_, bf16[1024,1024]{1,0:T(8,128)(2,1)} %get-tuple-element.9.refs_2_.refs_4_, ...), custom_call_target="tpu_custom_call" | custom-call | tf_op jit(solution)/shard_map/apply/pallas_call | solution.py:287
  (1 shorter events, 0.0 us)
Async XLA Ops:
  6.5 89.6 %all-gather.7.cloned.1.call-start = ((), (), s32[]{:S(2)}) async-start(), calls=%async_computation.1 | async-start | bytes 4460544 | tf_op jit(solution)/shard_map/all_gather | solution.py:231
  10.6 167.7 %all-gather.5.cloned.1.call-start = ((), (), s32[]{:S(2)}) async-start(), calls=%async_computation | async-start | bytes 9437184 | tf_op jit(solution)/shard_map/all_gather | solution.py:234
  14.4 145.1 %copy-start = (f32[256,1024]{1,0:T(8,128)}, f32[256,1024]{1,0:T(8,128)S(1)}, u32[]{:S(2)}) copy-start(f32[256,1024]{1,0:T(8,128)S(1)} %pad_maximum_fusion.refs_9_) | copy-start | bytes 3145732
  14.4 145.1 %collective-permute-start.2 = (f32[256,1024]{1,0:T(8,128)S(1)}, f32[256,1024]{1,0:T(8,128)S(1)}, u32[]{:S(2)}, u32[]{:S(2)}) collective-permute-start(f32[256,1024]{1,0:T(8,128)S(1)} %pad_maximum_fusion.refs_9_), channel_id=1, source_target_pairs={{0,8},{8,16},{16,24},{24,0},{1,9},{9,17},{17,25},{25,1},{2,10},{10... | collective-permute-start | bytes 3145736 | tf_op jit(solution)/shard_map/ppermute | solution.py:236
  17.4 142.1 %collective-permute-start.1 = (f32[256,1024]{1,0:T(8,128)S(1)}, f32[256,1024]{1,0:T(8,128)S(1)}, u32[]{:S(2)}, u32[]{:S(2)}) collective-permute-start(f32[256,1024]{1,0:T(8,128)S(1)} %pad_maximum_fusion.refs_9_), channel_id=1, source_target_pairs={{0,16},{8,24},{16,0},{24,8},{1,17},{9,25},{17,1},{25,9},{2,18},{10... | collective-permute-start | bytes 3145736 | tf_op jit(solution)/shard_map/ppermute | solution.py:236
  18.9 140.6 %collective-permute-start = (f32[256,1024]{1,0:T(8,128)S(1)}, f32[256,1024]{1,0:T(8,128)}, u32[]{:S(2)}, u32[]{:S(2)}) collective-permute-start(f32[256,1024]{1,0:T(8,128)S(1)} %pad_maximum_fusion.refs_9_), channel_id=1, source_target_pairs={{0,24},{8,0},{16,8},{24,16},{1,25},{9,1},{17,9},{25,17},{2,26},{10... | collective-permute-start | bytes 3145736 | tf_op jit(solution)/shard_map/ppermute | solution.py:236
  159.5 18.9 %copy-start.1 = (f32[256,1024]{1,0:T(8,128)}, f32[256,1024]{1,0:T(8,128)S(1)}, u32[]{:S(2)}) copy-start(f32[256,1024]{1,0:T(8,128)S(1)} %collective-permute-done.2.refs_12_) | copy-start | bytes 3145732
  159.5 18.9 %copy-start.2 = (f32[256,1024]{1,0:T(8,128)}, f32[256,1024]{1,0:T(8,128)S(1)}, u32[]{:S(2)}) copy-start(f32[256,1024]{1,0:T(8,128)S(1)} %collective-permute-done.1.refs_11_) | copy-start | bytes 3145732
Sparse Core Ops, SparseCore 0:
  10.8 85.2 all-gather.6
  97.7 80.5 all-gather.4
